TPU v7x, 32 devices: a whole 2x2x4 slice. The times are simulated.
32 devices in a mesh: dp: 16 (over z, y, x), mp: 2 (over core).
Axes of the slice: x: 2, y: 2, z: 4, core: 2. Of those that a mesh axis runs over, the one named last changes fastest.
Arguments:
- grad: bfloat16 [4, 1024, 8192], P(None, 'dp', 'mp'), may hold values from -6 to 6
- second_moment: float32 [4, 1024, 8192], P(None, 'dp', 'mp'), may hold values from 0.004 to 20, as said below
- left_root: bfloat16 [2, 16, 1024, 1024], P('mp', 'dp'), as said below
- right_root: bfloat16 [2, 16, 1024, 1024], P('mp', 'dp'), as said below
- owner_slot: int32 [2, 4, 4], replicated, may hold values from 0 to 15, as said below
Outputs:
- update: bfloat16 [4, 1024, 8192], P(None, 'dp', 'mp')
Inputs may be any that keep to these rules, and one draw needn't show every extreme that they name: For each h, owner_slot[h] lists every dp index exactly once: each dp index owns one block of each h. `second_moment`: positive. `left_root`: each square is symmetric positive definite. `right_root`: each square is symmetric positive definite.
All inputs are finite; a program needn't handle non-finite values.
Results may differ from a plain program's by a relative error of at most 0.0049.
Values may be sent and summed in bfloat16 or wider, within the bound.
A program may use at most 64 MiB of HBM per device.

v0:
```python
import jax
import jax.numpy as jnp
from jax import lax
from jax.sharding import PartitionSpec as P

BETA_TWO = 0.99
ADAM_EPS = 1e-08
NORM_EPS = 1e-06


def per_device(grad, second_moment, left_root, right_root, owner_slot):
    row_blocks, block_rows, half_cols = grad.shape
    block_size = left_root.shape[-1]
    col_blocks = half_cols // block_size
    dp_count = lax.axis_size("dp")
    mp_index = lax.axis_index("mp")
    widened = grad.astype(jnp.float32)
    moment_new = BETA_TWO * second_moment + (1.0 - BETA_TWO) * widened * widened
    direction = widened / (jnp.sqrt(moment_new) + ADAM_EPS)
    partial_value = jnp.sum(
        (direction * direction).reshape(row_blocks, block_rows, col_blocks, block_size), axis=(1, 3)
    )
    table = lax.dynamic_index_in_dim(owner_slot, mp_index, 0, keepdims=False)
    owner_ids = lax.iota(jnp.int32, dp_count)
    matches = table[None, :, :] == owner_ids[:, None, None]
    select_half = matches.astype(jnp.bfloat16)
    select_full = matches.astype(jnp.float32).reshape(dp_count, row_blocks * col_blocks)
    tiles = grad.reshape(row_blocks, block_rows, col_blocks, block_size)
    outgoing = jnp.einsum("src,rwck->swk", select_half, tiles, preferred_element_type=jnp.float32)
    outgoing = outgoing.astype(jnp.bfloat16).reshape(dp_count, 1, block_rows, block_size)
    per_owner = jnp.dot(select_full, partial_value.reshape(-1), precision=lax.Precision.HIGHEST)
    arrived_sq = lax.all_to_all(per_owner, "dp", split_axis=0, concat_axis=0, tiled=True)
    adam_sq = jnp.sum(arrived_sq)
    left = left_root[0, 0]
    right = right_root[0, 0]
    arrived = lax.all_to_all(outgoing, "dp", split_axis=0, concat_axis=1, tiled=True)
    block = arrived.reshape(block_size, block_size)
    mixed = jnp.dot(block, right, preferred_element_type=jnp.float32).astype(jnp.bfloat16)
    shaped = jnp.dot(left, mixed, preferred_element_type=jnp.float32)
    shaped_sq = jnp.sum(shaped * shaped)
    factor = jnp.sqrt((adam_sq + NORM_EPS) / (shaped_sq + NORM_EPS))
    result = (shaped * factor).astype(jnp.bfloat16).reshape(1, dp_count, block_rows, block_size)
    back = lax.all_to_all(result, "dp", split_axis=1, concat_axis=0, tiled=True)
    placed = jnp.einsum(
        "src,swk->rwck",
        select_half,
        back.reshape(dp_count, block_rows, block_size),
        preferred_element_type=jnp.float32,
    )
    return placed.astype(jnp.bfloat16).reshape(row_blocks, block_rows, half_cols)


def solution(mesh):
    in_specs = (
        P(None, "dp", "mp"),
        P(None, "dp", "mp"),
        P("mp", "dp", None, None),
        P("mp", "dp", None, None),
        P(),
    )
    out_specs = P(None, "dp", "mp")
    return jax.shard_map(
        per_device, mesh=mesh, in_specs=in_specs, out_specs=out_specs, check_vma=False
    )
```

profile of v0, /device:TPU:0, one launch (start us, length us, event | category | flops | bytes accessed | tf_op | source)
XLA Modules:
  0.0 157.1 jit_solution(964478429440768154)
XLA Ops:
  0.0 0.0 copy-start
  0.0 0.0 copy-start.1
  0.0 5.4 %fusion.4 = f32[4,4096]{1,0:T(4,128)S(1)} fusion(f32[4,64,4096]{2,1,0:T(8,128)} %param.6, bf16[4,64,4096]{2,1,0:T(8,128)(2,1)} %param.5), kind=kLoop, calls=%fused_computation.9 | loop fusion | flops 9420800 | bytes 6356992 | tf_op jit(solution)/shard_map/reduce_sum | solution.py:20
  5.4 0.1 reduce_sum.35
  5.5 0.0 copy-done.1
  5.5 0.1 reduce_sum.36
  5.6 0.9 fusion.21
  6.5 8.3 %all-to-all-start.1 = ((f32[16,1,1]{2,1,0:T(1,128)}), f32[16,1,1]{2,1,0:T(1,128)S(1)}, u32[]{:S(2)}, u32[]{:S(2)}) async-start(f32[16,1,1]{2,1,0:T(1,128)} %bitcast.24), calls=%async_computation.1 | async-start | bytes 16384 | tf_op jit(solution)/shard_map/all_to_all | solution.py:32
  14.9 4.5 %reshape.32 = bf16[4,64,4,1024]{3,2,1,0:T(4,128)(2,1)} reshape(bf16[4,64,4096]{2,1,0:T(8,128)(2,1)} %param.5) | data formatting | bytes 4194304 | tf_op jit(solution)/shard_map/reshape | solution.py:28
  19.4 3.2 %fusion.15 = bf16[16,1,64,1024]{3,0,2,1:T(8,128)(2,1)S(1)} fusion(bf16[4,64,4,1024]{3,2,1,0:T(4,128)(2,1)} %reshape.32, s32[4,4]{1,0:T(4,128)S(1)} %dynamic-slice_bitcast_fusion), kind=kOutput, calls=%fused_computation.19 | convolution fusion | flops 34603264 | bytes 4194368 | tf_op jit(solution)/shard_map/src,rwck->swk/dot_general | solution.py:29
  22.6 2.5 %copy.22 = bf16[16,1,64,1024]{3,2,1,0:T(8,128)(2,1)} copy(bf16[16,1,64,1024]{3,0,2,1:T(8,128)(2,1)S(1)} %fusion.15) | data formatting | bytes 4194304 | tf_op jit(solution)/shard_map/reshape | solution.py:30
  25.1 0.0 all-to-all-done.1
  25.1 7.0 %all-to-all-start = ((bf16[16,1,64,1024]{3,2,1,0:T(8,128)(2,1)}), bf16[16,1,64,1024]{3,2,1,0:T(8,128)(2,1)}, u32[]{:S(2)}, u32[]{:S(2)}) async-start(bf16[16,1,64,1024]{3,2,1,0:T(8,128)(2,1)} %copy.22), calls=%async_computation | async-start | bytes 4194304 | tf_op jit(solution)/shard_map/all_to_all | solution.py:36
  32.0 0.7 reduce_sum.37
  33.4 41.4 %all-to-all-done = bf16[16,1,64,1024]{3,2,1,0:T(8,128)(2,1)} async-done(((bf16[16,1,64,1024]{3,2,1,0:T(8,128)(2,1)}), bf16[16,1,64,1024]{3,2,1,0:T(8,128)(2,1)}, u32[]{:S(2)}, u32[]{:S(2)}) %all-to-all-start) | async-done | bytes 2097184 | tf_op jit(solution)/shard_map/all_to_all | solution.py:36
  74.8 0.0 copy-done
  74.8 9.2 %multiply_reduce_fusion = (f32[]{:T(128)}, f32[1024,1024]{0,1:T(8,128)}) fusion(bf16[1024,1024]{1,0:T(8,128)(2,1)} %bitcast.5, bf16[1,1,1024,1024]{3,2,1,0:T(8,128)(2,1)S(1)} %copy-done, bf16[1,1,1024,1024]{3,2,1,0:T(8,128)(2,1)} %param.7), kind=kOutput, calls=%fused_computation.8 | convolution fusion | flops 4298113024 | bytes 10485764 | tf_op jit(solution)/shard_map/dot_general | solution.py:39
  84.8 2.8 %multiply_convert_fusion = bf16[1024,1024]{0,1:T(8,128)(2,1)S(1)} fusion(f32[1024,1024]{0,1:T(8,128)} %get-tuple-element.6, f32[]{:T(128)S(6)} %sqrt.7), kind=kLoop, calls=%fused_computation.7 | loop fusion | flops 2097152 | bytes 6291460 | tf_op jit(solution)/shard_map/convert_element_type | solution.py:42
  87.6 57.9 %all_to_all.27 = bf16[1,16,64,1024]{3,2,0,1:T(8,128)(2,1)S(1)} all-to-all(bf16[1,16,64,1024]{3,2,0,1:T(8,128)(2,1)S(1)} %bitcast.60), channel_id=1, replica_groups=mesh['dp'=16,'mp'=2] {'dp'}, dimensions={1} | all-to-all | bytes 4194304 | tf_op jit(solution)/shard_map/all_to_all | solution.py:43
  145.4 3.1 %convert_bitcast_fusion = bf16[4,64,4,1024]{3,2,0,1:T(4,128)(2,1)} fusion(bf16[1,16,64,1024]{3,2,0,1:T(8,128)(2,1)S(1)} %all_to_all.27, s32[4,4]{1,0:T(4,128)S(1)} %dynamic-slice_bitcast_fusion), kind=kOutput, calls=%fused_computation.17 | convolution fusion | flops 34603264 | bytes 4194368 | tf_op jit(solution)/shard_map/src,swk->rwck/dot_general | solution.py:44
  148.5 4.5 %reshape.37 = bf16[4,64,4096]{2,0,1:T(4,128)(2,1)} reshape(bf16[4,64,4,1024]{3,2,0,1:T(4,128)(2,1)} %convert_bitcast_fusion) | data formatting | bytes 4194304 | tf_op jit(solution)/shard_map/reshape | solution.py:50
  153.0 4.1 %copy.26 = bf16[4,64,4096]{2,1,0:T(8,128)(2,1)} copy(bf16[4,64,4096]{2,0,1:T(4,128)(2,1)} %reshape.37) | data formatting | bytes 4194304 | tf_op jit(solution)/shard_map/reshape | solution.py:50
  (1 shorter events, 0.0 us)
Async XLA Ops:
  0.0 74.8 %copy-start = (bf16[1,1,1024,1024]{3,2,1,0:T(8,128)(2,1)S(1)}, bf16[1,1,1024,1024]{3,2,1,0:T(8,128)(2,1)}, u32[]{:S(2)}) copy-start(bf16[1,1,1024,1024]{3,2,1,0:T(8,128)(2,1)} %param.8) | copy-start | bytes 6291460
  0.0 5.5 %copy-start.1 = (s32[2,4,4]{2,1,0:T(4,128)S(1)}, s32[2,4,4]{2,1,0:T(4,128)}, u32[]{:S(2)}) copy-start(s32[2,4,4]{2,1,0:T(4,128)} %param.9) | copy-start | bytes 388
  6.5 18.6 %all-to-all-start.1 = ((f32[16,1,1]{2,1,0:T(1,128)}), f32[16,1,1]{2,1,0:T(1,128)S(1)}, u32[]{:S(2)}, u32[]{:S(2)}) async-start(f32[16,1,1]{2,1,0:T(1,128)} %bitcast.24), calls=%async_computation.1 | async-start | bytes 16384 | tf_op jit(solution)/shard_map/all_to_all | solution.py:32
  25.1 49.7 %all-to-all-start = ((bf16[16,1,64,1024]{3,2,1,0:T(8,128)(2,1)}), bf16[16,1,64,1024]{3,2,1,0:T(8,128)(2,1)}, u32[]{:S(2)}, u32[]{:S(2)}) async-start(bf16[16,1,64,1024]{3,2,1,0:T(8,128)(2,1)} %copy.22), calls=%async_computation | async-start | bytes 4194304 | tf_op jit(solution)/shard_map/all_to_all | solution.py:36
where the time goes:
time: 158 us; the launch traced here: 157 us
  blocking collectives  57.9 us (37%)
  waiting for transfers between devices  41.4 us (26%)
  matrix products  16.5 us (10%)
  local copies, waits for them, and re-layouts  15.6 us (10%)
  starting transfers between devices  15.3 us (10%)
  other arithmetic  8.99 us (6%)
    all_to_all x1, blocking collectives, per_device(): back = lax.all_to_all(result, 'dp', split_axis=1, concat_axis=0, tiled=True)  57.9 us
    all_to_all x1, waiting for transfers between devices, per_device(): lax.all_to_all(outgoing, 'dp', split_axis=0, concat_axis=1, tiled=True)  41.4 us
    dot_general x1, matrix products, per_device(): shaped = jnp.dot(left, mixed, preferred_element_type=jnp.float32)  9.24 us
    reshape x2, local copies, waits for them, and re-layouts, per_device(): placed.astype(jnp.bfloat16).reshape(row_blocks, block_rows, half_cols)  8.57 us
    all_to_all x1, starting transfers between devices, per_device(): lax.all_to_all(per_owner, 'dp', split_axis=0, concat_axis=0, tiled=True)  8.34 us
    all_to_all x1, starting transfers between devices, per_device(): lax.all_to_all(outgoing, 'dp', split_axis=0, concat_axis=1, tiled=True)  6.96 us
    reduce_sum x2, other arithmetic, per_device(): jnp.sum((direction * direction).reshape(row_blocks, block_rows, col_block...  5.52 us
    reshape x1, local copies, waits for them, and re-layouts, per_device(): tiles = grad.reshape(row_blocks, block_rows, col_blocks, block_size)  4.49 us
  transfers between devices with their start and end apart: 2, of which 1 were waited for; matrix products, arithmetic and copies ran while one was open for 7% of the time, Pallas kernels for 0%

commit v1 on v0

v1 whole, which is shorter than its diff:
```python
import functools

import jax
import jax.numpy as jnp
from jax import lax
from jax.experimental import pallas as pl
from jax.experimental.pallas import tpu as pltpu
from jax.sharding import PartitionSpec as P

BETA_TWO = 0.99
ADAM_EPS = 1e-08
NORM_EPS = 1e-06

LANES = 128
GROUP_ROWS = 256


def xor(a, k, n):
    value, bit = 0, 1
    while bit < n:
        value = value + ((a // bit + k // bit) % 2) * bit
        bit *= 2
    return value


def exchange_kernel(
    n, block_of, grad_hbm, moment_hbm, left_hbm, right_hbm, back,
    grad, moment, left, right, staged, arrived, mixed, total, result,
    parts, parts_out, parts_in,
    local_sem, grad_sem, send_sem, recv_sem, part_send, part_recv, back_send, back_recv,
):
    rows = grad.shape[1]
    size = left.shape[0]
    col_blocks = grad_hbm.shape[2] // size
    groups = max(size // GROUP_ROWS, 1)
    group = n // groups
    group_rows = size // groups
    me = lax.axis_index("dp")
    my_group, my_place = me // group, me % group
    send_order = [g for g in reversed(range(groups)) if g >= groups // 2]
    send_order = sorted(send_order)
    late_order = [g for g in reversed(range(groups)) if g < groups // 2]
    take_order = [g for g in range(groups // 2)] + send_order[::-1]

    def base_of(g):
        return xor(my_group, g, groups) * group

    def partner(g, j):
        return base_of(g) + (my_place + j) % group

    def over(g, body):
        def step(j, carry):
            body(partner(g, j))
            return carry

        lax.fori_loop(1 if g == 0 else 0, group, step, 0)

    barrier = pltpu.get_barrier_semaphore()
    for g in range(groups):
        over(g, lambda d: pl.semaphore_signal(barrier, inc=1, device_id={"dp": d}))

    def grad_load(b):
        cols = pl.ds(pl.multiple_of((b % col_blocks) * size, size), size)
        return pltpu.make_async_copy(
            grad_hbm.at[b // col_blocks, :, cols], grad.at[b], grad_sem.at[b]
        )

    def grad_start(b, carry):
        grad_load(b).start()
        return carry

    def grad_wait(b, carry):
        grad_load(b).wait()
        return carry

    lax.fori_loop(0, n, grad_start, 0)
    loads = [
        pltpu.make_async_copy(src, dst, local_sem.at[i])
        for i, (src, dst) in enumerate(
            [(moment_hbm, moment), (right_hbm.at[0, 0], right), (left_hbm.at[0, 0], left)]
        )
    ]
    for load in loads:
        load.start()

    def own_rows(s):
        return grad[block_of[s]]

    def chunk_copy(d):
        return pltpu.make_async_remote_copy(
            src_ref=staged.at[d], dst_ref=arrived.at[me], send_sem=send_sem.at[d],
            recv_sem=recv_sem.at[me], device_id={"dp": d},
        )

    def chunk_from(s):
        return pltpu.make_async_remote_copy(
            src_ref=staged.at[s], dst_ref=arrived.at[s], send_sem=send_sem.at[s],
            recv_sem=recv_sem.at[s], device_id={"dp": s},
        )

    def part_copy(d):
        return pltpu.make_async_remote_copy(
            src_ref=parts_out.at[d], dst_ref=parts_in.at[me], send_sem=part_send.at[d],
            recv_sem=part_recv.at[me], device_id={"dp": d},
        )

    def part_from(s):
        return pltpu.make_async_remote_copy(
            src_ref=parts_out.at[s], dst_ref=parts_in.at[s], send_sem=part_send.at[s],
            recv_sem=part_recv.at[s], device_id={"dp": s},
        )

    def back_copy(d):
        return pltpu.make_async_remote_copy(
            src_ref=result.at[d], dst_ref=back.at[me], send_sem=back_send.at[d],
            recv_sem=back_recv.at[me], device_id={"dp": d},
        )

    def back_from(s):
        return pltpu.make_async_remote_copy(
            src_ref=result.at[s], dst_ref=back.at[s], send_sem=back_send.at[s],
            recv_sem=back_recv.at[s], device_id={"dp": s},
        )

    def stage(d):
        staged[d] = own_rows(d)

    lax.fori_loop(0, n, grad_wait, 0)
    for g in send_order:
        over(g, stage)
    pl.semaphore_wait(barrier, n - 1)
    for g in send_order:
        over(g, lambda d: chunk_copy(d).start())
    for g in late_order:
        over(g, stage)
    arrived[me] = own_rows(me)
    loads[0].wait()

    piece = 2 * LANES

    def adam(b, carry):
        r, c = b // col_blocks, b % col_blocks
        sums = jnp.zeros((1, piece), jnp.float32)
        for p in range(size // piece):
            cols = pl.ds(pl.multiple_of(c * size + p * piece, piece), piece)
            widened = grad[b, :, p * piece : (p + 1) * piece].astype(jnp.float32)
            moment_new = BETA_TWO * moment[r, :, cols] + (1.0 - BETA_TWO) * widened * widened
            direction = widened / (jnp.sqrt(moment_new) + ADAM_EPS)
            sums = sums + jnp.sum(direction * direction, axis=0, keepdims=True)
        parts[b] = sums[:, :LANES] + sums[:, LANES:]
        return carry

    lax.fori_loop(0, n, adam, 0)

    def stage_part(d):
        parts_out[d] = parts[block_of[d]]

    for g in range(groups):
        over(g, stage_part)
    parts_in[me] = parts[block_of[me]]
    for g in send_order + late_order:
        over(g, lambda d: part_copy(d).start())
    for g in late_order:
        over(g, lambda d: chunk_copy(d).start())
    loads[1].wait()
    loads[2].wait()

    col_tile = min(size, 256)
    row_tile = min(size, 256)
    squares = jnp.zeros((8, size), jnp.float32)
    for position, g in enumerate(take_order):
        over(g, lambda s: chunk_from(s).wait_recv())
        base = base_of(g)

        def mix(t, carry):
            block = arrived[pl.ds(base, group)]
            if rows % 16 != 0:
                block = block.astype(jnp.float32)
            block = block.reshape(group_rows, size).astype(jnp.bfloat16)
            cols = pl.ds(pl.multiple_of(t * col_tile, col_tile), col_tile)
            mixed[:, cols] = jnp.dot(
                block, right[:, cols], preferred_element_type=jnp.float32
            ).astype(jnp.bfloat16)
            return carry

        lax.fori_loop(0, size // col_tile, mix, 0)
        depth = pl.ds(pl.multiple_of(base * rows, group_rows), group_rows)
        last = position == groups - 1

        def shape(t, sums):
            tile = pl.ds(pl.multiple_of(t * row_tile, row_tile), row_tile)
            term = jnp.dot(left[tile, depth], mixed[...], preferred_element_type=jnp.float32)
            if position > 0:
                term = total[tile, :] + term
            total[tile, :] = term
            if last:
                sums = sums + jnp.sum((term * term).reshape(row_tile // 8, 8, size), axis=0)
            return sums

        squares = lax.fori_loop(0, size // row_tile, shape, squares)

    for g in range(groups):
        over(g, lambda s: part_from(s).wait_recv())
    shaped_sq = jnp.sum(jnp.sum(squares, axis=0, keepdims=True), axis=1, keepdims=True)
    adam_sq = jnp.sum(jnp.sum(parts_in[...], axis=0), axis=1, keepdims=True)
    factor = jnp.sqrt((adam_sq + NORM_EPS) / (shaped_sq + NORM_EPS))

    def finish(d):
        tile = pl.ds(pl.multiple_of(d * rows, rows), rows)
        result[d] = (total[tile, :] * factor).astype(jnp.bfloat16)

    for g in send_order + late_order:
        over(g, finish)
        over(g, lambda d: back_copy(d).start())
    finish(me)
    own = pltpu.make_async_copy(result.at[me], back.at[me], local_sem.at[0])
    own.start()
    for g in range(groups):
        over(g, lambda d: chunk_copy(d).wait_send())
        over(g, lambda d: part_copy(d).wait_send())
    own.wait()
    for g in range(groups):
        over(g, lambda d: back_copy(d).wait_send())
        over(g, lambda s: back_from(s).wait_recv())


def place_kernel(n, table, back, out, held, in_sem, out_sem):
    col_blocks = out.shape[2] // back.shape[2]
    size = back.shape[2]
    half = lax.axis_index("mp")

    def fetch(b):
        owner = table[half, b // col_blocks, b % col_blocks]
        return pltpu.make_async_copy(back.at[owner], held.at[b], in_sem.at[b])

    def put(b):
        cols = pl.ds(pl.multiple_of((b % col_blocks) * size, size), size)
        return pltpu.make_async_copy(held.at[b], out.at[b // col_blocks, :, cols], out_sem.at[b])

    def first(b, carry):
        fetch(b).start()
        return carry

    def second(b, carry):
        fetch(b).wait()
        put(b).start()
        return carry

    def third(b, carry):
        put(b).wait()
        return carry

    lax.fori_loop(0, n, first, 0)
    lax.fori_loop(0, n, second, 0)
    lax.fori_loop(0, n, third, 0)


def per_device(grad, second_moment, left_root, right_root, owner_slot):
    row_blocks, rows, half_cols = grad.shape
    size = left_root.shape[-1]
    n = lax.axis_size("dp")
    group_rows = size // max(size // GROUP_ROWS, 1)
    smem = pl.BlockSpec(memory_space=pltpu.SMEM)
    anywhere = pl.BlockSpec(memory_space=pl.ANY)
    chunks = (n, rows, size)
    table = lax.dynamic_index_in_dim(owner_slot, lax.axis_index("mp"), 0, keepdims=False).reshape(-1)
    ids = lax.iota(jnp.int32, n)
    matches = table[None, :] == ids[:, None]
    block_of = jnp.sum(jnp.where(matches, ids[None, :], 0), axis=1)
    back = pl.pallas_call(
        functools.partial(exchange_kernel, n),
        out_shape=jax.ShapeDtypeStruct(chunks, jnp.bfloat16),
        in_specs=[smem] + [anywhere] * 4,
        out_specs=anywhere,
        scratch_shapes=[
            pltpu.VMEM(chunks, grad.dtype),
            pltpu.VMEM(second_moment.shape, jnp.float32),
            pltpu.VMEM((size, size), jnp.bfloat16),
            pltpu.VMEM((size, size), jnp.bfloat16),
            pltpu.VMEM(chunks, jnp.bfloat16),
            pltpu.VMEM(chunks, jnp.bfloat16),
            pltpu.VMEM((group_rows, size), jnp.bfloat16),
            pltpu.VMEM((size, size), jnp.float32),
            pltpu.VMEM(chunks, jnp.bfloat16),
            pltpu.VMEM((n, 1, LANES), jnp.float32),
            pltpu.VMEM((n, 1, LANES), jnp.float32),
            pltpu.VMEM((n, 1, LANES), jnp.float32),
            pltpu.SemaphoreType.DMA((3,)),
            pltpu.SemaphoreType.DMA((n,)),
        ]
        + [pltpu.SemaphoreType.DMA((n,))] * 6,
        compiler_params=pltpu.CompilerParams(collective_id=0, has_side_effects=True),
    )(block_of, grad, second_moment, left_root, right_root)
    return pl.pallas_call(
        functools.partial(place_kernel, n),
        out_shape=jax.ShapeDtypeStruct(grad.shape, jnp.bfloat16),
        in_specs=[smem, anywhere],
        out_specs=anywhere,
        scratch_shapes=[
            pltpu.VMEM(chunks, jnp.bfloat16),
            pltpu.SemaphoreType.DMA((n,)),
            pltpu.SemaphoreType.DMA((n,)),
        ],
    )(owner_slot, back)


def solution(mesh):
    in_specs = (
        P(None, "dp", "mp"),
        P(None, "dp", "mp"),
        P("mp", "dp", None, None),
        P("mp", "dp", None, None),
        P(),
    )
    out_specs = P(None, "dp", "mp")
    return jax.shard_map(
        per_device, mesh=mesh, in_specs=in_specs, out_specs=out_specs, check_vma=False
    )
```

time: 158 us -> 107 us (0.68)
  the two profiles are of different devices: /device:TPU:0 before, /device:TPU:19 now
where the time goes in v1:
time: 107 us
  Pallas kernels  105 us (98%)
    pallas_call x1, Pallas kernels, per_device(): pl.pallas_call(functools.partial(exchange_kernel, n), out_shape=jax.Shape...  102 us
    pallas_call x1, Pallas kernels, per_device(): pl.pallas_call(functools.partial(place_kernel, n), out_shape=jax.ShapeDty...  3.32 us

profile of v1, /device:TPU:19, one launch (start us, length us, event | category | flops | bytes accessed | tf_op | source)
XLA Modules:
  0.0 106.6 jit_solution(11713860210574865254)
XLA Ops:
  0.0 0.7 constant_dynamic-slice_fusion
  0.7 0.1 eq.15
  0.8 0.6 select_reduce_fusion.block_of
  1.4 101.9 %shard_map.55.back = bf16[16,64,1024]{2,1,0:T(8,128)(2,1)} custom-call(s32[16]{0:T(128)} %select_reduce_fusion.block_of, bf16[4,64,4096]{2,1,0:T(8,128)(2,1)} %grad_hbm.1, f32[4,64,4096]{2,1,0:T(8,128)} %moment_hbm.1, bf16[1,1,1024,1024]{3,2,1,0:T(8,128)(2,1)} %left_hbm.1, bf16[1,1,1024,1024]{3,2,1,0:T(8,128)(2,1)} %right_hbm.1), custom_call_target="tpu_custom_call" | custom-call | tf_op jit(solution)/shard_map/pallas_call | solution.py:270
  103.3 3.3 %shard_map.56 = bf16[4,64,4096]{2,1,0:T(8,128)(2,1)} custom-call(s32[2,4,4]{2,1,0:T(4,128)} %table.1, bf16[16,64,1024]{2,1,0:T(8,128)(2,1)} %shard_map.55.back), custom_call_target="tpu_custom_call" | custom-call | tf_op jit(solution)/shard_map/pallas_call | solution.py:294

commit v2 on v1

--- a/solution.py
+++ b/solution.py
@@ -13,6 +13,12 @@
 
 LANES = 128
 GROUP_ROWS = 256
+VMEM_LIMIT = 48 * 1024 * 1024
+FIRST = [1]
+CROSS = [2, 3]
+REST = [0]
+BACK = [1, 2, 3, 0]
+SKEW = True
 
 
 def xor(a, k, n):
@@ -36,11 +42,9 @@
     group = n // groups
     group_rows = size // groups
     me = lax.axis_index("dp")
+    half = lax.axis_index("mp")
     my_group, my_place = me // group, me % group
-    send_order = [g for g in reversed(range(groups)) if g >= groups // 2]
-    send_order = sorted(send_order)
-    late_order = [g for g in reversed(range(groups)) if g < groups // 2]
-    take_order = [g for g in range(groups // 2)] + send_order[::-1]
+    take_order = [0, 1] + CROSS
 
     def base_of(g):
         return xor(my_group, g, groups) * group
@@ -84,7 +88,7 @@
         load.start()
 
     def own_rows(s):
-        return grad[block_of[s]]
+        return grad[block_of[half, s]]
 
     def chunk_copy(d):
         return pltpu.make_async_remote_copy(
@@ -125,14 +129,16 @@
     def stage(d):
         staged[d] = own_rows(d)
 
+    def send(gs):
+        for g in gs:
+            over(g, lambda d: chunk_copy(d).start())
+
     lax.fori_loop(0, n, grad_wait, 0)
-    for g in send_order:
+    for g in FIRST + CROSS + REST:
         over(g, stage)
     pl.semaphore_wait(barrier, n - 1)
-    for g in send_order:
-        over(g, lambda d: chunk_copy(d).start())
-    for g in late_order:
-        over(g, stage)
+    pl.when(half == 0)(lambda: send(CROSS))
+    send(FIRST + REST)
     arrived[me] = own_rows(me)
     loads[0].wait()
 
@@ -153,15 +159,13 @@
     lax.fori_loop(0, n, adam, 0)
 
     def stage_part(d):
-        parts_out[d] = parts[block_of[d]]
+        parts_out[d] = parts[block_of[half, d]]
 
     for g in range(groups):
         over(g, stage_part)
-    parts_in[me] = parts[block_of[me]]
-    for g in send_order + late_order:
+    parts_in[me] = parts[block_of[half, me]]
+    for g in range(groups):
         over(g, lambda d: part_copy(d).start())
-    for g in late_order:
-        over(g, lambda d: chunk_copy(d).start())
     loads[1].wait()
     loads[2].wait()
 
@@ -169,6 +173,8 @@
     row_tile = min(size, 256)
     squares = jnp.zeros((8, size), jnp.float32)
     for position, g in enumerate(take_order):
+        if SKEW and g == CROSS[0]:
+            pl.when(half != 0)(lambda: send(CROSS))
         over(g, lambda s: chunk_from(s).wait_recv())
         base = base_of(g)
 
@@ -209,50 +215,39 @@
         tile = pl.ds(pl.multiple_of(d * rows, rows), rows)
         result[d] = (total[tile, :] * factor).astype(jnp.bfloat16)
 
-    for g in send_order + late_order:
+    for g in BACK:
         over(g, finish)
         over(g, lambda d: back_copy(d).start())
-    finish(me)
-    own = pltpu.make_async_copy(result.at[me], back.at[me], local_sem.at[0])
-    own.start()
+    tile = pl.ds(pl.multiple_of(me * rows, rows), rows)
+    back[me] = (total[tile, :] * factor).astype(jnp.bfloat16)
     for g in range(groups):
         over(g, lambda d: chunk_copy(d).wait_send())
         over(g, lambda d: part_copy(d).wait_send())
-    own.wait()
     for g in range(groups):
         over(g, lambda d: back_copy(d).wait_send())
         over(g, lambda s: back_from(s).wait_recv())
 
 
-def place_kernel(n, table, back, out, held, in_sem, out_sem):
-    col_blocks = out.shape[2] // back.shape[2]
+def place_kernel(n, table, back, out, sem):
     size = back.shape[2]
+    col_blocks = out.shape[2] // size
     half = lax.axis_index("mp")
 
-    def fetch(b):
+    def put(b):
         owner = table[half, b // col_blocks, b % col_blocks]
-        return pltpu.make_async_copy(back.at[owner], held.at[b], in_sem.at[b])
-
-    def put(b):
         cols = pl.ds(pl.multiple_of((b % col_blocks) * size, size), size)
-        return pltpu.make_async_copy(held.at[b], out.at[b // col_blocks, :, cols], out_sem.at[b])
-
-    def first(b, carry):
-        fetch(b).start()
-        return carry
-
-    def second(b, carry):
-        fetch(b).wait()
+        return pltpu.make_async_copy(back.at[owner], out.at[b // col_blocks, :, cols], sem.at[b])
+
+    def start(b, carry):
         put(b).start()
         return carry
 
-    def third(b, carry):
+    def wait(b, carry):
         put(b).wait()
         return carry
 
-    lax.fori_loop(0, n, first, 0)
-    lax.fori_loop(0, n, second, 0)
-    lax.fori_loop(0, n, third, 0)
+    lax.fori_loop(0, n, start, 0)
+    lax.fori_loop(0, n, wait, 0)
 
 
 def per_device(grad, second_moment, left_root, right_root, owner_slot):
@@ -261,17 +256,19 @@
     n = lax.axis_size("dp")
     group_rows = size // max(size // GROUP_ROWS, 1)
     smem = pl.BlockSpec(memory_space=pltpu.SMEM)
-    anywhere = pl.BlockSpec(memory_space=pl.ANY)
+    hbm = pl.BlockSpec(memory_space=pltpu.HBM)
+    vmem = pl.BlockSpec(memory_space=pltpu.VMEM)
     chunks = (n, rows, size)
-    table = lax.dynamic_index_in_dim(owner_slot, lax.axis_index("mp"), 0, keepdims=False).reshape(-1)
-    ids = lax.iota(jnp.int32, n)
-    matches = table[None, :] == ids[:, None]
-    block_of = jnp.sum(jnp.where(matches, ids[None, :], 0), axis=1)
+    col_blocks = owner_slot.shape[2]
+    block_ids = lax.broadcasted_iota(jnp.int32, (1, 1) + owner_slot.shape[1:], 2) * col_blocks
+    block_ids = block_ids + lax.broadcasted_iota(jnp.int32, (1, 1) + owner_slot.shape[1:], 3)
+    matches = owner_slot[:, None] == lax.iota(jnp.int32, n)[None, :, None, None]
+    block_of = jnp.sum(jnp.where(matches, block_ids, 0), axis=(2, 3))
     back = pl.pallas_call(
         functools.partial(exchange_kernel, n),
-        out_shape=jax.ShapeDtypeStruct(chunks, jnp.bfloat16),
-        in_specs=[smem] + [anywhere] * 4,
-        out_specs=anywhere,
+        out_shape=pltpu.VMEM(chunks, jnp.bfloat16),
+        in_specs=[smem] + [hbm] * 4,
+        out_specs=vmem,
         scratch_shapes=[
             pltpu.VMEM(chunks, grad.dtype),
             pltpu.VMEM(second_moment.shape, jnp.float32),
@@ -289,18 +286,17 @@
             pltpu.SemaphoreType.DMA((n,)),
         ]
         + [pltpu.SemaphoreType.DMA((n,))] * 6,
-        compiler_params=pltpu.CompilerParams(collective_id=0, has_side_effects=True),
+        compiler_params=pltpu.CompilerParams(
+            collective_id=0, has_side_effects=True, vmem_limit_bytes=VMEM_LIMIT
+        ),
     )(block_of, grad, second_moment, left_root, right_root)
     return pl.pallas_call(
         functools.partial(place_kernel, n),
         out_shape=jax.ShapeDtypeStruct(grad.shape, jnp.bfloat16),
-        in_specs=[smem, anywhere],
-        out_specs=anywhere,
-        scratch_shapes=[
-            pltpu.VMEM(chunks, jnp.bfloat16),
-            pltpu.SemaphoreType.DMA((n,)),
-            pltpu.SemaphoreType.DMA((n,)),
-        ],
+        in_specs=[smem, vmem],
+        out_specs=hbm,
+        scratch_shapes=[pltpu.SemaphoreType.DMA((n,))],
+        compiler_params=pltpu.CompilerParams(vmem_limit_bytes=VMEM_LIMIT),
     )(owner_slot, back)
 
 

time: 107 us -> 104 us (0.972)
  Pallas kernels: 105 us -> 101 us
    pallas_call x1, Pallas kernels: 102 us -> 99.4 us  [per_device(): pl.pallas_call(functools.partial(exchange_kernel, n), out_shape=pltpu.VME...]
    unnamed x0 -> x4, local copies, waits for them, and re-layouts: none -> 1.59 us
    pallas_call x1, Pallas kernels: 3.32 us -> 2.06 us  [per_device(): pl.pallas_call(functools.partial(place_kernel, n), out_shape=jax.ShapeDty...]
where the time goes in v2:
time: 104 us
  Pallas kernels  101 us (97%)
  local copies, waits for them, and re-layouts  1.59 us (2%)
    pallas_call x1, Pallas kernels, per_device(): pl.pallas_call(functools.partial(exchange_kernel, n), out_shape=pltpu.VME...  99.4 us

profile of v2, /device:TPU:19, one launch (start us, length us, event | category | flops | bytes accessed | tf_op | source)
XLA Modules:
  0.0 103.9 jit_solution(1787011455938643573)
XLA Ops:
  0.0 0.1 iota_add_fusion
  0.1 0.8 select_reduce_fusion.block_of
  0.9 0.0 copy-start
  0.9 1.6 %copy-done = bf16[4,64,4096]{2,1,0:T(8,128)(2,1)S(1)} copy-done((bf16[4,64,4096]{2,1,0:T(8,128)(2,1)S(1)}, bf16[4,64,4096]{2,1,0:T(8,128)(2,1)}, u32[]{:S(2)}) %copy-start) | copy-done | bytes 2097176
  2.5 0.0 copy-start.1
  2.5 99.4 %shard_map.55.back = bf16[16,64,1024]{2,1,0:T(8,128)(2,1)S(1)} custom-call(s32[2,16]{1,0:T(2,128)S(1)} %select_reduce_fusion.block_of, bf16[4,64,4096]{2,1,0:T(8,128)(2,1)S(1)} %copy-done, f32[4,64,4096]{2,1,0:T(8,128)} %moment_hbm.1, bf16[1,1,1024,1024]{3,2,1,0:T(8,128)(2,1)} %left_hbm.1, bf16[1,1,1024,1024]{3,2,1,0:T(8,128)(2,1)} %right_hbm.1), custom_call_target="tpu_custom_call" | custom-call | tf_op jit(solution)/shard_map/pallas_call | solution.py:267
  101.9 0.0 copy-done.1
  101.9 2.1 %shard_map.56 = bf16[4,64,4096]{2,1,0:T(8,128)(2,1)} custom-call(s32[2,4,4]{2,1,0:T(4,128)S(1)} %copy-done.1, bf16[16,64,1024]{2,1,0:T(8,128)(2,1)S(1)} %shard_map.55.back), custom_call_target="tpu_custom_call" | custom-call | tf_op jit(solution)/shard_map/pallas_call | solution.py:293
  (1 shorter events, 0.0 us)
Async XLA Ops:
  0.9 1.6 %copy-start = (bf16[4,64,4096]{2,1,0:T(8,128)(2,1)S(1)}, bf16[4,64,4096]{2,1,0:T(8,128)(2,1)}, u32[]{:S(2)}) copy-start(bf16[4,64,4096]{2,1,0:T(8,128)(2,1)} %grad_hbm.1) | copy-start | bytes 6291460
  2.5 99.4 %copy-start.1 = (s32[2,4,4]{2,1,0:T(4,128)S(1)}, s32[2,4,4]{2,1,0:T(4,128)}, u32[]{:S(2)}) copy-start(s32[2,4,4]{2,1,0:T(4,128)} %table.1) | copy-start | bytes 388
